TPU v7x, 128 devices: a whole 4x4x4 slice. The times are simulated.
128 devices in a mesh: dp: 32 (over x, z, core), tensor: 4 (over y).
Axes of the slice: x: 4, y: 4, z: 4, core: 2. Of those that a mesh axis runs over, the one named last changes fastest.
Arguments:
- tokens: bfloat16 [16384, 4096], P(('dp', 'tensor')), may hold values from -6 to 6
- norm_gain: float32 [4096], replicated, may hold values from 0.1 to 1.9
- w_query: bfloat16 [4096, 2048], P(None, 'tensor'), may hold values from -2 to 2
- key_weight: bfloat16 [4096, 512], P(None, 'tensor'), may hold values from -0.09375 to 0.09375
- value_weight: bfloat16 [4096, 512], P(None, 'tensor'), may hold values from -0.09375 to 0.09375
- w_out: bfloat16 [2048, 4096], P('tensor'), may hold values from -0.125 to 0.125
- lengths: int32 [16], replicated, may hold values from 1 to 8704, 16384 in all
Outputs:
- layer_out: bfloat16 [16384, 4096], P(('dp', 'tensor'))
Inputs may be any that keep to these rules, and one draw needn't show every extreme that they name: The lengths sum to 16384, and some document has exactly 8704 tokens.
All inputs are finite; a program needn't handle non-finite values.
Results may differ from a plain program's by a relative error of at most 0.0095.
The roundings to bfloat16 on the way count: a program that leaves them out, or rounds other values in their place, can miss the bound.
Values may be sent and summed in bfloat16 or wider, within the bound.
No kernel may reach another device: no remote copies, remote signals or barrier semaphores. Data moves between devices by JAX's collectives and lax.ppermute only.
A program may use at most 128 MiB of HBM per device.

v0:
```python
import jax
import jax.numpy as jnp
from jax import lax
from jax.sharding import PartitionSpec as P

HEAD_SIZE = 128


epsilon = 1e-05
rope_base = 500000.0
masked = -1e30
initial_peak = -1e29


def in_one_piece(arrays, axis, dim, along):
    ends, at = ([], 0)
    for a in arrays[:-1]:
        at += a.shape[along]
        ends.append(at)
    both = jnp.concatenate(arrays, axis=along)
    return tuple(jnp.split(lax.all_gather(both, axis, axis=dim, tiled=True), ends, axis=along))


def doc_starts(lengths, positions):
    doc_ends = jnp.cumsum(lengths)
    closed = (doc_ends[None, :] <= positions[:, None]).astype(jnp.int32)
    return jnp.sum(closed * lengths[None, :], axis=1)


def rotate(vectors, offsets):
    half_width = vectors.shape[-1] // 2
    exponent = jnp.arange(half_width, dtype=jnp.float32) * (-2.0 / vectors.shape[-1])
    frequency = rope_base**exponent
    angles = offsets.astype(jnp.float32)[:, None] * frequency[None, :]
    cos_part = jnp.cos(angles)[:, None, :]
    sin_part = jnp.sin(angles)[:, None, :]
    leading = vectors[..., :half_width]
    trailing = vectors[..., half_width:]
    return jnp.concatenate(
        [leading * cos_part - trailing * sin_part, trailing * cos_part + leading * sin_part],
        axis=-1,
    )


def project(tokens, norm_gain, w_query, key_weight, value_weight, positions, starts):
    count = tokens.shape[0]
    wide = tokens.astype(jnp.float32)
    inverse = lax.rsqrt(jnp.mean(wide * wide, axis=1, keepdims=True) + epsilon)
    normed = (wide * inverse * norm_gain[None, :]).astype(jnp.bfloat16)
    offsets = positions - starts
    query_rows = jnp.dot(normed, w_query, preferred_element_type=jnp.float32).reshape(
        count, -1, HEAD_SIZE
    )
    query_rows = rotate(query_rows, offsets).astype(jnp.bfloat16)
    key = jnp.dot(normed, key_weight, preferred_element_type=jnp.float32).reshape(
        count, -1, HEAD_SIZE
    )
    key = rotate(key, offsets).astype(jnp.bfloat16)
    value_rows = jnp.dot(normed, value_weight, preferred_element_type=jnp.float32).astype(
        jnp.bfloat16
    )
    return (query_rows, key.reshape(count, -1), value_rows)


def attend_block(carry, keys, values, first_key, context):
    query_rows, positions, starts = context
    length = keys.shape[0]
    heads = query_rows.shape[1]
    key_pos = first_key + jnp.arange(length, dtype=jnp.int32)
    useful = (first_key + length - 1 >= starts[0]) & (first_key <= positions[-1])
    scale = query_rows.shape[-1] ** (-0.5)

    def compute(state):
        peak, mass, summed = state
        key_view = keys.reshape(length, heads, -1)
        value_view = values.reshape(length, heads, -1)
        scores = (
            jnp.einsum("qkgd,skd->qkgs", query_rows, key_view, preferred_element_type=jnp.float32)
            * scale
        )
        visible = (key_pos[None, :] >= starts[:, None]) & (key_pos[None, :] <= positions[:, None])
        scores = jnp.where(visible[:, None, None, :], scores, masked)
        fresh = jnp.maximum(peak, jnp.max(scores, axis=-1))
        shrink = jnp.exp(peak - fresh)
        probs = jnp.exp(scores - fresh[..., None])
        mass = mass * shrink + jnp.sum(probs, axis=-1)
        update = jnp.einsum(
            "qkgs,skd->qkgd",
            probs.astype(jnp.bfloat16),
            value_view,
            preferred_element_type=jnp.float32,
        )
        summed = summed * shrink[..., None] + update
        return (fresh, mass, summed)

    def unchanged(state):
        return state

    return lax.cond(useful, compute, unchanged, carry)


def fold_keys(carry, pieces, context):
    keys, values = pieces
    width = keys.shape[0]
    size = min(width, 1024)
    whole = width // size

    def one_block(index, state):
        offset = (index * size).astype(jnp.int32)
        key_part = lax.dynamic_slice_in_dim(keys, offset, size, 0)
        value_part = lax.dynamic_slice_in_dim(values, offset, size, 0)
        return attend_block(state, key_part, value_part, offset, context)

    carry = lax.fori_loop(0, whole, one_block, carry)
    return carry


def body(tokens, norm_gain, w_query, key_weight, value_weight, w_out, lengths):
    gathered = lax.all_gather(tokens, "tensor", axis=0, tiled=True)
    count = gathered.shape[0]
    first = lax.axis_index("dp") * count
    positions = first + jnp.arange(count, dtype=jnp.int32)
    starts = doc_starts(lengths, positions)
    query_rows, key, value_rows = project(
        gathered, norm_gain, w_query, key_weight, value_weight, positions, starts
    )
    heads = key.shape[1] // HEAD_SIZE
    query_rows = query_rows.reshape(count, heads, -1, HEAD_SIZE)
    group_count = query_rows.shape[2]
    context = (query_rows, positions, starts)
    initial = (
        jnp.full((count, heads, group_count), initial_peak, jnp.float32),
        jnp.zeros((count, heads, group_count), jnp.float32),
        jnp.zeros((count, heads, group_count, HEAD_SIZE), jnp.float32),
    )
    carry = fold_keys(initial, in_one_piece((key, value_rows), "dp", 0, 1), context)
    peak, mass, summed = carry
    attended = (summed / mass[..., None]).reshape(count, -1).astype(jnp.bfloat16)
    branch = lax.psum_scatter(
        jnp.dot(attended, w_out, preferred_element_type=jnp.float32).astype(jnp.bfloat16),
        "tensor",
        scatter_dimension=0,
        tiled=True,
    ).astype(jnp.float32)
    return (tokens.astype(jnp.float32) + branch).astype(jnp.bfloat16)


def solution(mesh):
    in_specs = (
        P(("dp", "tensor"), None),
        P(),
        P(None, "tensor"),
        P(None, "tensor"),
        P(None, "tensor"),
        P("tensor", None),
        P(),
    )
    out_specs = P(("dp", "tensor"), None)
    return jax.shard_map(body, mesh=mesh, in_specs=in_specs, out_specs=out_specs, check_vma=False)
```

profile of v0, /device:TPU:1, one launch (start us, length us, event | category | flops | bytes accessed | tf_op | source)
XLA Modules:
  0.0 327.9 jit_solution(13975362636619700645)
XLA Ops:
  6.5 0.7 all-gather.3.cloned.1.call-update
  7.3 0.7 copy.19
  8.2 0.7 select_reduce_fusion
  9.0 51.3 %all-gather.3.cloned.1.call-done = bf16[512,4096]{1,0:T(8,128)(2,1)} async-done(((bf16[128,4096]{1,0:T(8,128)(2,1)}), bf16[512,4096]{1,0:T(8,128)(2,1)}) %all-gather.3.cloned.1.call-update) | async-done | bytes 4194320 | tf_op jit(solution)/shard_map/all_gather | solution.py:119
  60.3 3.2 fusion.24
  63.7 1.6 convolution_bitcast_fusion
  65.9 1.6 convolution_convert_fusion.1
  67.5 0.7 pad_maximum_fusion.1
  68.5 1.8 multiply_cosine_fusion
  70.3 5.9 %fusion.39 = f32[512,512]{0,1:T(8,128)S(1)} fusion(bf16[4096,512]{1,0:T(8,128)(2,1)} %param.13, bf16[512,4096]{1,0:T(8,128)(2,1)} %all-gather.3.cloned.1.call-done, f32[4096]{0:T(1024)S(1)} %copy-done.4, f32[512]{0:T(512)S(1)} %add_rsqrt_fusion), kind=kOutput, calls=%fused_computation.61 | convolution fusion | flops 2155872256 | bytes 9455616 | tf_op jit(solution)/shard_map/dot_general | solution.py:51
  76.2 0.9 fusion.44
  77.5 1.4 copy.24
  78.9 1.2 fusion.27
  80.4 47.9 %all-gather.5.cloned.1.call-done = bf16[16384,256]{0,1:T(8,128)(2,1)} async-done(((bf16[512,256]{0,1:T(8,128)(2,1)}), bf16[16384,256]{0,1:T(8,128)(2,1)}) %all-gather.5.cloned.1.call-update) | async-done | bytes 8388624 | tf_op jit(solution)/shard_map/all_gather | solution.py:21
  128.3 5.8 %fusion.43 = (bf16[16384,128]{0,1:T(8,128)(2,1)}, bf16[16384,128]{0,1:T(8,128)(2,1)}) fusion(bf16[16384,256]{0,1:T(8,128)(2,1)} %all-gather.5.cloned.1.call-done), kind=kLoop, calls=%fused_computation.62 | loop fusion | bytes 16777216 | tf_op jit(solution)/shard_map/split | solution.py:21
  134.0 6.4 %copy.22 = bf16[16384,128]{1,0:T(8,128)(2,1)} copy(bf16[16384,128]{0,1:T(8,128)(2,1)} %get-tuple-element.495) | data formatting | bytes 8388608 | tf_op jit(solution)/shard_map/while | solution.py:114
  140.5 51.2 %while.21 = (s32[]{:T(128)}, f32[512,1,4]{0,2,1:T(4,128)S(1)}, f32[512,1,4]{0,2,1:T(4,128)S(1)}, f32[512,1,4,128]{0,3,2,1:T(8,128)S(1)}, s32[512]{0:T(512)S(1)},...) while((s32[]{:T(128)}, f32[512,1,4]{0,2,1:T(4,128)S(1)}, ...), condition=%wide.region_8.9_spmd, body=%wide.region_3.8_spmd.sunk | while | flops 1098914816 | bytes 30560620 | solution.py:114
  141.8 0.6 slice.63
  143.2 8.5 %conditional.2 = ((f32[512,1,4]{0,2,1:T(4,128)S(1)}, f32[512,1,4]{0,2,1:T(4,128)S(1)}, f32[512,1,4,128]{0,3,2,1:T(8,128)S(1)})) conditional(s32[]{:T(128)} %convert_element_type.108, (f32[512,1,4]{0,2,1:T(4,128)S(1)}, f32[512,1,4]{0,2,1:T(4,128)S(1)}, f32[512,1,4,128]{0,3,2,1:T(8,128)S(1)}) %tuple.77, (s32[]{:T(128)}, s32[1024]{0:T(1024)S(1)}, ...), branch_computations={%region_4.4_spmd, %region_5.7_spmd} | conditional | flops 1098914816 | bytes 30556238 | solution.py:99
  143.7 2.5 fusion.2
  146.2 3.5 %fusion.10 = f32[512,1,4,128]{0,3,2,1:T(8,128)S(1)} fusion(f32[1024,512,4]{1,0,2:T(8,128)S(1)} %get-tuple-element.493, f32[512,4]{0,1:T(4,128)S(1)} %bitcast.76, pred[512,1024]{0,1:T(8,128)(4,1)S(1)} %compare_and_fusion, f32[512,1,4,128]{0,3,2,1:T(8,128)S(1)} %get-tuple-element.426, f32[512,4]{0,1:T(4,128)S(1)} %get-tuple-element.490, ...), kind=kOutput, calls=%fused_computation.10 | convolution fusion | flops 545783808 | bytes 11288580 | tf_op jit(solution)/shard_map/while/body/eval_jaxpr/cond/branch_1_fun/qkgs,skd->qkgd/dot_general | solution.py:87
  149.8 1.8 fusion.1
  152.9 0.6 slice.63
  158.2 0.6 slice.63
  160.9 0.6 slice.63
  163.5 0.6 slice.63
  166.2 0.6 slice.63
  171.5 0.6 slice.63
  174.2 0.6 slice.63
  191.8 6.5 %convolution_convert_fusion = bf16[512,4096]{1,0:T(8,128)(2,1)} fusion(bf16[512,512]{0,1:T(8,128)(2,1)S(1)} %bitcast.78, bf16[512,4096]{1,0:T(8,128)(2,1)} %param.16), kind=kOutput, calls=%fused_computation.31 | convolution fusion | flops 2149580800 | bytes 8912896 | tf_op jit(solution)/shard_map/dot_general | solution.py:140
  198.4 120.6 %reduce-scatter.2.cloned.1.call-done = bf16[128,4096]{1,0:T(8,128)(2,1)} async-done(((bf16[512,4096]{1,0:T(8,128)(2,1)}), bf16[128,4096]{1,0:T(8,128)(2,1)}) %reduce-scatter.2.cloned.1.call-update) | async-done | bytes 1048592 | tf_op jit(solution)/shard_map/reduce_scatter | solution.py:139
  319.0 2.4 add_convert_fusion
  (88 shorter events, 17.3 us)
Async XLA Ops:
  6.5 57.0 %copy-start = (bf16[4096,128]{1,0:T(8,128)(2,1)S(1)}, bf16[4096,128]{1,0:T(8,128)(2,1)}, u32[]{:S(2)}) copy-start(bf16[4096,128]{1,0:T(8,128)(2,1)} %param.14) | copy-start | bytes 3145732
  6.5 57.0 %copy-start.4 = (f32[4096]{0:T(1024)S(1)}, f32[4096]{0:T(1024)}, u32[]{:S(2)}) copy-start(f32[4096]{0:T(1024)} %param.12) | copy-start | bytes 49156
  6.5 53.7 %all-gather.3.cloned.1.call-start = ((), (), s32[]{:S(2)}) async-start(), calls=%async_computation.1 | async-start | bytes 5242880 | tf_op jit(solution)/shard_map/all_gather | solution.py:119
  7.3 121.0 %all-gather.5.cloned.1.call-start = ((), (), s32[]{:S(2)}) async-start(), calls=%async_computation.2 | async-start | bytes 8650752 | tf_op jit(solution)/shard_map/all_gather | solution.py:21
  60.3 3.4 %copy-start.2 = (bf16[512,4096]{1,0:T(8,128)(2,1)S(1)}, bf16[512,4096]{1,0:T(8,128)(2,1)}, u32[]{:S(2)}) copy-start(bf16[512,4096]{1,0:T(8,128)(2,1)} %all-gather.3.cloned.1.call-done) | copy-start | bytes 12582916
  63.7 2.2 copy-start.3
  68.3 250.7 %reduce-scatter.2.cloned.1.call-start = ((), (), s32[]{:S(2)}) async-start(), calls=%async_computation.3 | async-start | bytes 5242880 | tf_op jit(solution)/shard_map/reduce_scatter | solution.py:139
  198.3 120.6 %copy-start.1 = (bf16[128,4096]{1,0:T(8,128)(2,1)S(1)}, bf16[128,4096]{1,0:T(8,128)(2,1)}, u32[]{:S(2)}) copy-start(bf16[128,4096]{1,0:T(8,128)(2,1)} %param.11) | copy-start | bytes 3145732
Sparse Core Ops, SparseCore 0:
  9.0 51.2 all-gather.2
  68.4 59.7 all-gather.4
  198.5 120.4 reduce-scatter.1
where the time goes:
time: 330 us; the launch traced here: 328 us
  waiting for transfers between devices  221 us (67%)
  local copies, waits for them, and re-layouts  35.5 us (11%)
  loops' own time  23.1 us (7%)
  matrix products  21.7 us (7%)
  other arithmetic  13.7 us (4%)
  between operations  13.2 us (4%)
    reduce_scatter x1, waiting for transfers between devices, body(): lax.psum_scatter(jnp.dot(attended, w_out, preferred_element_type=jnp.floa...  121 us
    all_gather x1, waiting for transfers between devices, body(): gathered = lax.all_gather(tokens, 'tensor', axis=0, tiled=True)  51.3 us
    all_gather x1, waiting for transfers between devices, in_one_piece(): lax.all_gather(both, axis, axis=dim, tiled=True)  47.9 us
    another operation x1, loops' own time, fold_keys(): carry = lax.fori_loop(0, whole, one_block, carry)  22.8 us
    slice x16, local copies, waits for them, and re-layouts, attend_block(): positions[-1]  10.4 us
    slice x16, local copies, waits for them, and re-layouts, attend_block(): starts[0]  9.25 us
  transfers between devices with their start and end apart: 3, of which 3 were waited for; matrix products, arithmetic and copies ran while one was open for 4% of the time, Pallas kernels for 0%

commit v1 on v0

v1 whole, which is shorter than its diff:
```python
import functools

import jax
import jax.numpy as jnp
from jax import lax
from jax.experimental import pallas as pl
from jax.experimental.pallas import tpu as pltpu
from jax.sharding import PartitionSpec as P

HEAD_SIZE = 128


epsilon = 1e-05
rope_base = 500000.0
masked = -1e30
initial_peak = -1e29
KEY_BLOCK = 1024
ROWS = 256
exp2_scale = 1.4426950408889634 * HEAD_SIZE ** (-0.5)


def doc_starts(lengths, positions):
    doc_ends = jnp.cumsum(lengths)
    closed = (doc_ends[None, :] <= positions[:, None]).astype(jnp.int32)
    return jnp.sum(closed * lengths[None, :], axis=1)


def rotate(vectors, offsets):
    half_width = vectors.shape[-1] // 2
    exponent = jnp.arange(half_width, dtype=jnp.float32) * (-2.0 / vectors.shape[-1])
    frequency = rope_base**exponent
    angles = offsets.astype(jnp.float32)[:, None] * frequency[None, :]
    cos_part = jnp.cos(angles)[:, None, :]
    sin_part = jnp.sin(angles)[:, None, :]
    leading = vectors[..., :half_width]
    trailing = vectors[..., half_width:]
    return jnp.concatenate(
        [leading * cos_part - trailing * sin_part, trailing * cos_part + leading * sin_part],
        axis=-1,
    )


def project(tokens, norm_gain, w_query, key_weight, value_weight, positions, starts):
    count = tokens.shape[0]
    wide = tokens.astype(jnp.float32)
    inverse = lax.rsqrt(jnp.mean(wide * wide, axis=1, keepdims=True) + epsilon)
    normed = (wide * inverse * norm_gain[None, :]).astype(jnp.bfloat16)
    offsets = positions - starts
    query_rows = jnp.dot(normed, w_query, preferred_element_type=jnp.float32).reshape(
        count, -1, HEAD_SIZE
    )
    query_rows = rotate(query_rows, offsets).astype(jnp.bfloat16)
    key = jnp.dot(normed, key_weight, preferred_element_type=jnp.float32).reshape(
        count, -1, HEAD_SIZE
    )
    key = rotate(key, offsets).astype(jnp.bfloat16)
    value_rows = jnp.dot(normed, value_weight, preferred_element_type=jnp.float32).astype(
        jnp.bfloat16
    )
    return (query_rows.reshape(count, -1), key.reshape(count, -1), value_rows)


def attend_kernel(bounds, query, starts, kv, out, rows, peak, summed):
    first, low, high, full_low, full_high = [bounds[i] for i in range(5)]
    count = query.shape[0]
    heads = query.shape[1] // HEAD_SIZE
    size = KEY_BLOCK
    for h in range(heads):
        rows[h * count : (h + 1) * count, :] = query[:, h * HEAD_SIZE : (h + 1) * HEAD_SIZE]
    peak[...] = jnp.full(peak.shape, initial_peak, jnp.float32)
    summed[...] = jnp.zeros(summed.shape, jnp.float32)

    def step(index, cut):
        offset = pl.multiple_of(index * size, size)
        keys = kv[pl.ds(offset, size), :HEAD_SIZE]
        values = kv[pl.ds(offset, size), HEAD_SIZE:]
        values = jnp.concatenate([values, jnp.ones((size, HEAD_SIZE), jnp.bfloat16)], axis=1)
        for r in range(heads * count // ROWS):
            at = slice(r * ROWS, (r + 1) * ROWS)
            scores = lax.dot_general(
                rows[at, :], keys, (((1,), (1,)), ((), ())), preferred_element_type=jnp.float32
            )
            if cut:
                local = (r * ROWS) % count
                here = slice(local, local + ROWS)
                key_pos = offset + lax.broadcasted_iota(jnp.int32, (ROWS, size), 1)
                query_pos = first + local + lax.broadcasted_iota(jnp.int32, (ROWS, size), 0)
                visible = (key_pos >= starts[here, :]) & (key_pos <= query_pos)
                scores = jnp.where(visible, scores, masked)
            parts = [scores[:, c : c + HEAD_SIZE] for c in range(0, size, HEAD_SIZE)]
            old = peak[at, :]
            best = functools.reduce(jnp.maximum, parts)
            fresh = jnp.maximum(old, jnp.max(best, axis=1, keepdims=True))
            peak[at, :] = fresh
            shrink = jnp.exp2((old - fresh) * exp2_scale)
            probs = [jnp.exp2((part - fresh) * exp2_scale).astype(jnp.bfloat16) for part in parts]
            update = jnp.dot(
                jnp.concatenate(probs, axis=1), values, preferred_element_type=jnp.float32
            )
            summed[at, :HEAD_SIZE] = summed[at, :HEAD_SIZE] * shrink + update[:, :HEAD_SIZE]
            summed[at, HEAD_SIZE:] = summed[at, HEAD_SIZE:] * shrink + update[:, HEAD_SIZE:]

    def one_block(index, carry):
        whole = (index >= full_low) & (index < full_high)

        @pl.when(whole)
        def _():
            step(index, False)

        @pl.when(jnp.logical_not(whole))
        def _():
            step(index, True)

        return carry

    lax.fori_loop(low, high, one_block, 0)
    for h in range(heads):
        at = slice(h * count, (h + 1) * count)
        attended = summed[at, :HEAD_SIZE] / summed[at, HEAD_SIZE:]
        out[:, h * HEAD_SIZE : (h + 1) * HEAD_SIZE] = attended.astype(jnp.bfloat16)


def attend(query, kv, starts, first):
    count, width = query.shape
    rows = count * width // HEAD_SIZE
    size = KEY_BLOCK
    bounds = jnp.stack(
        [
            first,
            starts[0] // size,
            (first + count - 1) // size + 1,
            (starts[-1] + size - 1) // size,
            (first + 1) // size,
        ]
    ).astype(jnp.int32)
    vmem = pl.BlockSpec(memory_space=pltpu.VMEM)
    return pl.pallas_call(
        attend_kernel,
        out_shape=jax.ShapeDtypeStruct((count, width), jnp.bfloat16),
        in_specs=[pl.BlockSpec(memory_space=pltpu.SMEM), vmem, vmem, vmem],
        out_specs=vmem,
        scratch_shapes=[
            pltpu.VMEM((rows, HEAD_SIZE), jnp.bfloat16),
            pltpu.VMEM((rows, HEAD_SIZE), jnp.float32),
            pltpu.VMEM((rows, 2 * HEAD_SIZE), jnp.float32),
        ],
        compiler_params=pltpu.CompilerParams(vmem_limit_bytes=56 * 2**20),
        cost_estimate=pl.CostEstimate(
            flops=rows * 8704 * 512, transcendentals=rows * 8704, bytes_accessed=8 << 20
        ),
        name="attend",
    )(bounds, query, starts[:, None], kv)


def body(tokens, norm_gain, w_query, key_weight, value_weight, w_out, lengths):
    gathered = lax.all_gather(tokens, "tensor", axis=0, tiled=True)
    count = gathered.shape[0]
    first = lax.axis_index("dp") * count
    positions = first + jnp.arange(count, dtype=jnp.int32)
    starts = doc_starts(lengths, positions)
    query_rows, key, value_rows = project(
        gathered, norm_gain, w_query, key_weight, value_weight, positions, starts
    )
    kv = lax.all_gather(jnp.concatenate([key, value_rows], axis=1), "dp", axis=0, tiled=True)
    attended = attend(query_rows, kv, starts, first)
    branch = lax.psum_scatter(
        jnp.dot(attended, w_out, preferred_element_type=jnp.float32).astype(jnp.bfloat16),
        "tensor",
        scatter_dimension=0,
        tiled=True,
    ).astype(jnp.float32)
    return (tokens.astype(jnp.float32) + branch).astype(jnp.bfloat16)


def solution(mesh):
    in_specs = (
        P(("dp", "tensor"), None),
        P(),
        P(None, "tensor"),
        P(None, "tensor"),
        P(None, "tensor"),
        P("tensor", None),
        P(),
    )
    out_specs = P(("dp", "tensor"), None)
    return jax.shard_map(body, mesh=mesh, in_specs=in_specs, out_specs=out_specs, check_vma=False)
```

time: 330 us -> 221 us (0.67)
  waiting for transfers between devices: 221 us -> 162 us
  local copies, waits for them, and re-layouts: 35.5 us -> 6.65 us
  loops' own time: 23.1 us -> 0 us
  Pallas kernels: 0 us -> 8.9 us
  matrix products: 21.7 us -> 13.9 us
    reduce_scatter x1, waiting for transfers between devices: 121 us -> 75.3 us  [body(): lax.psum_scatter(jnp.dot(attended, w_out, preferred_element_type=jnp.floa...]
    another operation x17 -> x0, loops' own time: 23.1 us -> none  [the longest x1 22.8 us: fold_keys(): carry = lax.fori_loop(0, whole, one_block, carry)]
    slice x32 -> x1, local copies, waits for them, and re-layouts: 19.6 us -> 0.61 us  [attend(): starts[-1] + size - 1]
    all_gather x1, waiting for transfers between devices: 47.9 us -> 35 us  [body(): lax.all_gather(jnp.concatenate([key, value_rows], axis=1), 'dp', axis=0,...]
    pallas_call x0 -> x1, Pallas kernels: none -> 8.9 us  [attend(): pl.pallas_call(attend_kernel, out_shape=jax.ShapeDtypeStruct((count, widt...]
    while x1 -> x0, local copies, waits for them, and re-layouts: 6.36 us -> none  [fold_keys(): carry = lax.fori_loop(0, whole, one_block, carry)]
    dot_general x2 -> x0, matrix products: 6.06 us -> none  [the longest x1 3.54 us: compute(): jnp.einsum('qkgs,skd->qkgd', probs.astype(jnp.bfloat16), value_view, pref...]
    split x1 -> x0, local copies, waits for them, and re-layouts: 5.78 us -> none  [in_one_piece(): jnp.split(lax.all_gather(both, axis, axis=dim, tiled=True), ends, axis=al...]
  transfers between devices with their start and end apart: 3 -> 3, of which waited for: 3 -> 3; matrix products, arithmetic and copies ran while one was open for 4% -> 8% of each run, Pallas kernels for 0% -> 0%
where the time goes in v1:
time: 221 us
  waiting for transfers between devices  162 us (73%)
  between operations  16.3 us (7%)
  matrix products  13.9 us (6%)
  other arithmetic  12.7 us (6%)
  Pallas kernels  8.9 us (4%)
  local copies, waits for them, and re-layouts  6.65 us (3%)
    reduce_scatter x1, waiting for transfers between devices, body(): lax.psum_scatter(jnp.dot(attended, w_out, preferred_element_type=jnp.floa...  75.3 us
    all_gather x1, waiting for transfers between devices, body(): gathered = lax.all_gather(tokens, 'tensor', axis=0, tiled=True)  51.3 us
    all_gather x1, waiting for transfers between devices, body(): lax.all_gather(jnp.concatenate([key, value_rows], axis=1), 'dp', axis=0,...  35 us
    pallas_call x1, Pallas kernels, attend(): pl.pallas_call(attend_kernel, out_shape=jax.ShapeDtypeStruct((count, widt...  8.9 us
    dot_general x1, matrix products, project(): jnp.dot(normed, w_query, preferred_element_type=jnp.float32)  5.99 us
    dot_general x1, matrix products, body(): jnp.dot(attended, w_out, preferred_element_type=jnp.float32)  5.32 us
  transfers between devices with their start and end apart: 3, of which 3 were waited for; matrix products, arithmetic and copies ran while one was open for 8% of the time, Pallas kernels for 0%

profile of v1, /device:TPU:1, one launch (start us, length us, event | category | flops | bytes accessed | tf_op | source)
XLA Modules:
  0.0 220.9 jit_solution(5932137004861006245)
XLA Ops:
  6.5 0.0 copy-start
  6.5 0.7 all-gather.3.cloned.1.call-update
  7.3 0.0 all-gather.5.cloned.1.call-start
  7.3 0.7 copy.17
  8.1 0.1 reduce
  8.2 0.7 select_reduce_fusion
  9.0 51.3 %all-gather.3.cloned.1.call-done = bf16[512,4096]{1,0:T(8,128)(2,1)} async-done(((bf16[128,4096]{1,0:T(8,128)(2,1)}), bf16[512,4096]{1,0:T(8,128)(2,1)}) %all-gather.3.cloned.1.call-update) | async-done | bytes 4194320 | tf_op jit(solution)/shard_map/all_gather | solution.py:156
  60.3 3.2 %fusion = f32[512]{0:T(512)S(1)} fusion(bf16[512,4096]{1,0:T(8,128)(2,1)} %all-gather.3.cloned.1.call-done), kind=kLoop, calls=%fused_computation.2 | loop fusion | flops 6290944 | bytes 4196352 | tf_op jit(solution)/shard_map/reduce_sum | solution.py:46
  63.5 0.2 copy-done.2
  63.7 1.3 convolution_bitcast_fusion
  65.0 1.2 fusion.12
  66.3 1.3 convolution_convert_fusion.1
  67.6 0.9 pad_maximum_fusion.1
  68.5 0.0 all-gather.5.cloned.1.call-update
  68.5 0.0 reduce-scatter.2.cloned.1.call-start
  68.5 0.6 fusion.18
  72.3 0.9 copy.22.starts
  73.2 0.6 stack.23.bounds
  73.8 1.7 multiply_cosine_fusion.1
  75.5 6.0 %fusion.15 = f32[512,512]{0,1:T(8,128)S(1)} fusion(bf16[4096,512]{1,0:T(8,128)(2,1)} %param.9, bf16[512,4096]{1,0:T(8,128)(2,1)} %all-gather.3.cloned.1.call-done, f32[4096]{0:T(1024)S(1)} %copy-done.5, f32[512]{0:T(512)S(1)} %add_rsqrt_fusion), kind=kOutput, calls=%fused_computation.33 | convolution fusion | flops 2155872256 | bytes 9455616 | tf_op jit(solution)/shard_map/dot_general | solution.py:49
  81.5 0.9 fusion.17
  82.4 0.4 copy.25
  82.8 1.4 copy.26
  84.2 1.5 subtract_convert_fusion
  85.7 0.7 pad_maximum_fusion
  86.5 0.9 copy.29
  87.3 35.0 %all-gather.5.cloned.1.call-done.kv = bf16[16384,256]{1,0:T(8,128)(2,1)} async-done(((bf16[512,256]{1,0:T(8,128)(2,1)}), bf16[16384,256]{1,0:T(8,128)(2,1)}) %all-gather.5.cloned.1.call-update) | async-done | bytes 8388624 | tf_op jit(solution)/shard_map/all_gather | solution.py:164
  122.4 8.9 %attend.1 = bf16[512,512]{1,0:T(8,128)(2,1)} custom-call(s32[5]{0:T(128)} %stack.23.bounds, bf16[512,512]{1,0:T(8,128)(2,1)} %bitcast.27, s32[512,1]{1,0:T(8,128)} %copy.22.starts, bf16[16384,256]{1,0:T(8,128)(2,1)} %all-gather.5.cloned.1.call-done.kv), custom_call_target="tpu_custom_call" | custom-call | flops 9126805504 | bytes 8388608 | tf_op jit(solution)/shard_map/attend/pallas_call | solution.py:137
  131.3 5.3 %convolution_convert_fusion = bf16[512,4096]{1,0:T(8,128)(2,1)} fusion(bf16[512,512]{1,0:T(8,128)(2,1)} %attend.1, bf16[512,4096]{1,0:T(8,128)(2,1)S(1)} %copy-done.3), kind=kOutput, calls=%fused_computation.5 | convolution fusion | flops 2149580800 | bytes 8912896 | tf_op jit(solution)/shard_map/dot_general | solution.py:167
  136.6 0.0 reduce-scatter.2.cloned.1.call-update
  136.6 75.3 %reduce-scatter.2.cloned.1.call-done = bf16[128,4096]{1,0:T(8,128)(2,1)} async-done(((bf16[512,4096]{1,0:T(8,128)(2,1)}), bf16[128,4096]{1,0:T(8,128)(2,1)}) %reduce-scatter.2.cloned.1.call-update) | async-done | bytes 1048592 | tf_op jit(solution)/shard_map/reduce_scatter | solution.py:166
  211.9 2.4 %add_convert_fusion = bf16[128,4096]{1,0:T(8,128)(2,1)} fusion(bf16[128,4096]{1,0:T(8,128)(2,1)} %reduce-scatter.2.cloned.1.call-done, bf16[128,4096]{1,0:T(8,128)(2,1)S(1)} %copy-done.1), kind=kLoop, calls=%fused_computation.6 | loop fusion | flops 2097152 | bytes 3145728 | tf_op jit(solution)/shard_map/convert_element_type | solution.py:172
  (16 shorter events, 0.1 us)
Async XLA Ops:
  6.5 57.0 %copy-start = (bf16[4096,128]{1,0:T(8,128)(2,1)S(1)}, bf16[4096,128]{1,0:T(8,128)(2,1)}, u32[]{:S(2)}) copy-start(bf16[4096,128]{1,0:T(8,128)(2,1)} %param.10) | copy-start | bytes 3145732
  6.5 57.0 %copy-start.5 = (f32[4096]{0:T(1024)S(1)}, f32[4096]{0:T(1024)}, u32[]{:S(2)}) copy-start(f32[4096]{0:T(1024)} %param.8) | copy-start | bytes 49156
  6.5 53.7 %all-gather.3.cloned.1.call-start = ((), (), s32[]{:S(2)}) async-start(), calls=%async_computation.1 | async-start | bytes 5242880 | tf_op jit(solution)/shard_map/all_gather | solution.py:156
  7.3 115.1 %all-gather.5.cloned.1.call-start = ((), (), s32[]{:S(2)}) async-start(), calls=%async_computation.2 | async-start | bytes 8650752 | tf_op jit(solution)/shard_map/all_gather | solution.py:164
  60.3 3.4 %copy-start.2 = (bf16[512,4096]{1,0:T(8,128)(2,1)S(1)}, bf16[512,4096]{1,0:T(8,128)(2,1)}, u32[]{:S(2)}) copy-start(bf16[512,4096]{1,0:T(8,128)(2,1)} %all-gather.3.cloned.1.call-done) | copy-start | bytes 12582916
  63.7 2.5 %copy-start.4 = (bf16[4096,128]{1,0:T(8,128)(2,1)S(1)}, bf16[4096,128]{1,0:T(8,128)(2,1)}, u32[]{:S(2)}) copy-start(bf16[4096,128]{1,0:T(8,128)(2,1)} %param.11) | copy-start | bytes 3145732
  68.5 143.4 %reduce-scatter.2.cloned.1.call-start = ((), (), s32[]{:S(2)}) async-start(), calls=%async_computation.3 | async-start | bytes 5242880 | tf_op jit(solution)/shard_map/reduce_scatter | solution.py:166
  122.4 8.9 %copy-start.3 = (bf16[512,4096]{1,0:T(8,128)(2,1)S(1)}, bf16[512,4096]{1,0:T(8,128)(2,1)}, u32[]{:S(2)}) copy-start(bf16[512,4096]{1,0:T(8,128)(2,1)} %param.12) | copy-start | bytes 12582916
  136.6 75.3 %copy-start.1 = (bf16[128,4096]{1,0:T(8,128)(2,1)S(1)}, bf16[128,4096]{1,0:T(8,128)(2,1)}, u32[]{:S(2)}) copy-start(bf16[128,4096]{1,0:T(8,128)(2,1)} %param.7) | copy-start | bytes 3145732
Sparse Core Ops, SparseCore 0:
  9.0 51.2 all-gather.2
  68.6 53.7 all-gather.4
  136.8 75.1 reduce-scatter.1
